TPU v7x, 16 devices: a 4x2x1 block of a 4x4x8 slice. The times are simulated.
16 devices in a mesh: dp: 2 (over y, z), wg: 8 (over x, core).
Axes of the slice: x: 4, y: 2, z: 1, core: 2. Of those that a mesh axis runs over, the one named last changes fastest.
The devices are a block of a 4x4x8 slice.
Arguments:
- hidden_in: bfloat16 [96, 384, 2048], P(('dp', 'wg')), parts along dimension 0
- ln_g: float32 [2, 2048], replicated
- ln_b: float32 [2, 2048], replicated
- w_qkv: bfloat16 [2, 2048, 3, 32, 64], P(None, 'wg')
- b_qkv: float32 [2, 3, 32, 64], replicated
- w_out: bfloat16 [2, 32, 64, 2048], P(None, None, None, 'wg')
- b_out: float32 [2, 2048], replicated
- w_up: bfloat16 [2, 2048, 8192], P(None, 'wg')
- b_up: float32 [2, 8192], replicated
- w_down: bfloat16 [2, 8192, 2048], P(None, None, 'wg')
- b_down: float32 [2, 2048], replicated
- lnf_g: float32 [2048], replicated
- lnf_b: float32 [2048], replicated
Outputs:
- output: bfloat16 [96, 384, 2048], P(('dp', 'wg')), parts along dimension 0
There are 2 independent parts. A program takes and returns all parts, laid end to end along the dimension named above; an argument that names none is the same for every part.
All inputs are finite; a program needn't handle non-finite values.
Results may differ from a plain program's by a relative error of at most 0.0107003.
Values are sent between devices in bfloat16 or wider.
A program may use at most 768 MiB of HBM per device.

v0:
```python
import jax
import jax.numpy as jnp
from jax import lax
from jax.sharding import PartitionSpec as P

EPS = 1e-5


def layer_norm(rows, gain, shift):
    centered = rows - rows.mean(axis=-1, keepdims=True)
    variance = (centered * centered).mean(axis=-1, keepdims=True)
    return centered * lax.rsqrt(variance + EPS) * gain + shift


def decoder_layer(hidden, norm_gain, norm_shift, qkv_weight, qkv_bias, out_weight, out_bias, up_weight, up_bias, down_weight, down_bias):
    seq_len = hidden.shape[1]
    head_dim = qkv_weight.shape[-1]
    normed = layer_norm(hidden.astype(jnp.float32), norm_gain, norm_shift).astype(jnp.bfloat16)
    qkv_all = jnp.einsum('btd,dshe->btshe', normed, qkv_weight, preferred_element_type=jnp.float32)
    qkv_all = (qkv_all + qkv_bias).astype(jnp.bfloat16)
    scores = jnp.einsum('bqhe,bkhe->bhqk', qkv_all[:, :, 0], qkv_all[:, :, 1], preferred_element_type=jnp.float32) * head_dim ** -0.5
    positions = jnp.arange(seq_len)
    causal = positions[:, None] >= positions[None, :]
    scores = jnp.where(causal, scores, -1e30)
    attn_probs = jax.nn.softmax(scores, axis=-1).astype(jnp.bfloat16)
    mixed = jnp.einsum('bhqk,bkhe->bqhe', attn_probs, qkv_all[:, :, 2], preferred_element_type=jnp.float32).astype(jnp.bfloat16)
    attn_proj = jnp.einsum('crif,ife->cre', mixed, out_weight, preferred_element_type=jnp.float32)
    up_proj = jnp.einsum('btd,df->btf', normed, up_weight, preferred_element_type=jnp.float32) + up_bias
    gelu_out = jax.nn.gelu(up_proj, approximate=True).astype(jnp.bfloat16)
    down_proj = jnp.einsum('btf,fd->btd', gelu_out, down_weight, preferred_element_type=jnp.float32)
    updated = hidden.astype(jnp.float32) + attn_proj + out_bias + down_proj + down_bias
    return updated.astype(jnp.bfloat16)


def solution(mesh):
    row_spec = P(('dp', 'wg'), None, None)

    def local_forward(hidden_in, ln_g, ln_b, w_qkv, b_qkv, w_out, b_out, w_up, b_up, w_down, b_down, lnf_g, lnf_b):
        hidden = hidden_in
        for layer in range(w_qkv.shape[0]):
            full_qkv = lax.all_gather(w_qkv[layer], 'wg', axis=0, tiled=True)
            full_out = lax.all_gather(w_out[layer], 'wg', axis=2, tiled=True)
            full_up = lax.all_gather(w_up[layer], 'wg', axis=0, tiled=True)
            full_down = lax.all_gather(w_down[layer], 'wg', axis=1, tiled=True)
            hidden = decoder_layer(hidden, ln_g[layer], ln_b[layer], full_qkv, b_qkv[layer], full_out, b_out[layer], full_up, b_up[layer], full_down, b_down[layer])
        return layer_norm(hidden.astype(jnp.float32), lnf_g, lnf_b).astype(jnp.bfloat16)

    in_specs = (row_spec, P(), P(), P(None, 'wg', None, None, None), P(), P(None, None, None, 'wg'), P(),
                P(None, 'wg', None), P(), P(None, None, 'wg'), P(), P(), P())
    return jax.shard_map(local_forward, mesh=mesh, in_specs=in_specs, out_specs=row_spec, check_vma=False)
```

profile of v0, /device:TPU:113, one launch (start us, length us, event | category | flops | bytes accessed | tf_op | source)
XLA Modules:
  0.0 1114.1 jit_solution(3947787355289793943)
XLA Ops:
  6.6 6.7 fusion.128
  13.4 6.1 fusion.127
  19.6 5.7 fusion.126
  30.0 5.0 convert_reduce_fusion.1
  35.1 6.3 fusion.52
  45.1 94.0 %all-gather.17.cloned.1.call-done = bf16[1,2048,3,32,64]{1,4,3,2,0:T(8,128)(2,1)} async-done(((bf16[1,256,3,32,64]{1,4,3,2,0:T(8,128)(2,1)}), bf16[1,2048,3,32,64]{1,4,3,2,0:T(8,128)(2,1)}) %all-gather.17.cloned.1.call-update) | async-done | bytes 25165840 | tf_op jit(solution)/shard_map/all_gather | solution.py:41
  139.1 77.9 %add_convert_fusion.1 = bf16[6,384,3,32,64]{1,4,3,2,0:T(8,128)(2,1)} fusion(f32[3,32,64]{2,1,0:T(8,128)S(1)} %get-tuple-element.14, bf16[1,2048,3,32,64]{1,4,3,2,0:T(8,128)(2,1)} %all-gather.17.cloned.1.call-done, bf16[6,384,2048]{2,1,0:T(8,128)(2,1)} %param.13, f32[2048]{0:T(1024)S(1)} %bitcast.182, f32[2048]{0:T(1024)S(1)} %bitcast.180, ...), kind=kOutput, calls=%fused_computation.33 | convolution fusion | flops 58038681600 | bytes 62973952 | tf_op jit(solution)/shard_map/btd,dshe->btshe/dot_general | solution.py:19
  217.1 38.3 %fusion.135 = f32[6,32,384]{2,1,0:T(8,128)S(1)} fusion(pred[384,384]{0,1:T(8,128)(4,1)S(1)} %iota_compare_fusion, bf16[6,384,3,32,64]{1,4,3,2,0:T(8,128)(2,1)} %add_convert_fusion.1), kind=kOutput, calls=%fused_computation.140 | convolution fusion | flops 3737125120 | bytes 19316736 | tf_op jit(solution)/shard_map/sub | solution.py:25
  255.5 50.0 %fusion.24 = bf16[6,32,64,384]{3,2,1,0:T(8,128)(2,1)} fusion(f32[6,32,384]{2,1,0:T(8,128)S(1)} %fusion.135, pred[384,384]{0,1:T(8,128)(4,1)S(1)} %iota_compare_fusion, bf16[6,384,3,32,64]{1,4,3,2,0:T(8,128)(2,1)} %add_convert_fusion.1), kind=kOutput, calls=%fused_computation.34 | convolution fusion | flops 7389388800 | bytes 38191104 | tf_op jit(solution)/shard_map/bhqk,bkhe->bqhe/dot_general | solution.py:26
  305.5 89.5 %fusion.36 = f32[6,384,8192]{2,1,0:T(8,128)} fusion(bf16[1,2048,8192]{2,1,0:T(8,128)(2,1)} %all-gather.21.cloned.1.call-done, bf16[6,384,2048]{2,1,0:T(8,128)(2,1)} %param.13, f32[2048]{0:T(1024)S(1)} %bitcast.183, f32[2048]{0:T(1024)S(1)} %bitcast.181, f32[6,384]{1,0:T(8,128)S(1)} %copy-done.15, f32[6,384]{1,0:T(8,128)S(1)} %copy-done.7), kind=kOutput, calls=%fused_computation.44 | convolution fusion | flops 77337722880 | bytes 118523904 | tf_op jit(solution)/shard_map/btd,df->btf/dot_general | solution.py:28
  395.0 61.0 %all-gather.23.cloned.1.call-done = bf16[1,8192,2048]{2,1,0:T(8,128)(2,1)} async-done(((bf16[1,8192,256]{2,1,0:T(8,128)(2,1)}), bf16[1,8192,2048]{2,1,0:T(8,128)(2,1)}) %all-gather.23.cloned.1.call-update) | async-done | bytes 33554448 | tf_op jit(solution)/shard_map/all_gather | solution.py:44
  456.0 104.2 %fusion.30 = f32[6,384,2048]{2,1,0:T(8,128)} fusion(f32[6,384,8192]{2,1,0:T(8,128)} %fusion.36, f32[8192]{0:T(1024)S(1)} %bitcast.171, bf16[1,8192,2048]{2,1,0:T(8,128)(2,1)} %all-gather.23.cloned.1.call-done), kind=kOutput, calls=%fused_computation.39 | convolution fusion | flops 77498155008 | bytes 127959040 | tf_op jit(solution)/shard_map/btf,fd->btd/dot_general | solution.py:30
  560.2 32.2 %convert_reduce_fusion = (f32[6,384]{1,0:T(8,128)S(1)}, bf16[6,384,2048]{2,1,0:T(8,128)(2,1)}) fusion(f32[2048]{0:T(1024)S(1)} %bitcast.179, f32[6,384,2048]{2,1,0:T(8,128)} %fusion.30, f32[2048]{0:T(1024)S(1)} %bitcast.178, bf16[1,32,64,2048]{3,2,1,0:T(8,128)(2,1)} %all-gather.19.cloned.1.call-done, bf16[6,32,64,384]{3,2,1,0:T(8,128)(2,1)} %fusion.24, ...), kind=kOutput, calls=%fused_computation.48 | convolution fusion | flops 19365099520 | bytes 55600128 | tf_op jit(solution)/shard_map/crif,ife->cre/dot_general | solution.py:27
  592.4 6.3 fusion.48
  598.7 63.5 %all-gather.29.cloned.1.call-done = bf16[1,2048,8192]{2,1,0:T(8,128)(2,1)} async-done(((bf16[1,256,8192]{2,1,0:T(8,128)(2,1)}), bf16[1,2048,8192]{2,1,0:T(8,128)(2,1)}) %all-gather.29.cloned.1.call-update) | async-done | bytes 33554448 | tf_op jit(solution)/shard_map/all_gather | solution.py:43
  662.2 89.3 %fusion.33 = f32[6,384,8192]{2,1,0:T(8,128)} fusion(bf16[1,2048,8192]{2,1,0:T(8,128)(2,1)} %all-gather.29.cloned.1.call-done, bf16[6,384,2048]{2,1,0:T(8,128)(2,1)} %get-tuple-element.26, f32[2048]{0:T(1024)S(1)} %bitcast.176, f32[2048]{0:T(1024)S(1)} %bitcast.174, f32[6,384]{1,0:T(8,128)S(1)} %add_rsqrt_fusion.1, f32[6,384]{1,0:T(8,128)S(1)} %broadcast_multiply_fusion.1), kind=kOutput, calls=%fused_computation.41 | convolution fusion | flops 77337722880 | bytes 118523904 | tf_op jit(solution)/shard_map/btd,df->btf/dot_general | solution.py:28
  751.5 35.5 %all-gather.25.cloned.1.call-done = bf16[1,2048,3,32,64]{1,4,3,2,0:T(8,128)(2,1)} async-done(((bf16[1,256,3,32,64]{1,4,3,2,0:T(8,128)(2,1)}), bf16[1,2048,3,32,64]{1,4,3,2,0:T(8,128)(2,1)}) %all-gather.25.cloned.1.call-update) | async-done | bytes 25165840 | tf_op jit(solution)/shard_map/all_gather | solution.py:41
  787.0 78.0 %add_convert_fusion = bf16[6,384,3,32,64]{1,4,3,2,0:T(8,128)(2,1)} fusion(f32[3,32,64]{2,1,0:T(8,128)S(1)} %copy-done.5, bf16[1,2048,3,32,64]{1,4,3,2,0:T(8,128)(2,1)} %all-gather.25.cloned.1.call-done, bf16[6,384,2048]{2,1,0:T(8,128)(2,1)} %get-tuple-element.26, f32[2048]{0:T(1024)S(1)} %bitcast.177, f32[2048]{0:T(1024)S(1)} %bitcast.175, ...), kind=kOutput, calls=%fused_computation.28 | convolution fusion | flops 58038681600 | bytes 62973952 | tf_op jit(solution)/shard_map/btd,dshe->btshe/dot_general | solution.py:19
  864.9 38.2 %fusion.136 = f32[6,32,384]{2,1,0:T(8,128)S(1)} fusion(pred[384,384]{0,1:T(8,128)(4,1)S(1)} %copy-done.2, bf16[6,384,3,32,64]{1,4,3,2,0:T(8,128)(2,1)} %add_convert_fusion), kind=kOutput, calls=%fused_computation.141 | convolution fusion | flops 3737125120 | bytes 19316736 | tf_op jit(solution)/shard_map/sub | solution.py:25
  903.2 49.9 %fusion.25 = bf16[6,32,64,384]{3,2,1,0:T(8,128)(2,1)} fusion(f32[6,32,384]{2,1,0:T(8,128)S(1)} %fusion.136, pred[384,384]{0,1:T(8,128)(4,1)S(1)} %copy-done.2, bf16[6,384,3,32,64]{1,4,3,2,0:T(8,128)(2,1)} %add_convert_fusion), kind=kOutput, calls=%fused_computation.35 | convolution fusion | flops 7389388800 | bytes 38191104 | tf_op jit(solution)/shard_map/bhqk,bkhe->bqhe/dot_general | solution.py:26
  953.1 104.2 %fusion.28 = f32[6,384,2048]{2,1,0:T(8,128)} fusion(f32[6,384,8192]{2,1,0:T(8,128)} %fusion.33, f32[8192]{0:T(1024)S(1)} %bitcast.170, bf16[1,8192,2048]{2,1,0:T(8,128)(2,1)} %all-gather.31.cloned.1.call-done), kind=kOutput, calls=%fused_computation.38 | convolution fusion | flops 77498155008 | bytes 127959040 | tf_op jit(solution)/shard_map/btf,fd->btd/dot_general | solution.py:30
  1057.4 32.3 %convert_reduce_fusion.2 = (f32[6,384]{1,0:T(8,128)S(1)}, bf16[6,384,2048]{2,1,0:T(8,128)(2,1)}) fusion(f32[2048]{0:T(1024)S(1)} %bitcast.173, f32[6,384,2048]{2,1,0:T(8,128)} %fusion.28, f32[2048]{0:T(1024)S(1)} %bitcast.172, bf16[1,32,64,2048]{3,2,1,0:T(8,128)(2,1)} %all-gather.27.cloned.1.call-done, bf16[6,32,64,384]{3,2,1,0:T(8,128)(2,1)} %fusion.25, ...), kind=kOutput, calls=%fused_computation.57 | convolution fusion | flops 19365099520 | bytes 55600128 | tf_op jit(solution)/shard_map/crif,ife->cre/dot_general | solution.py:27
  1089.7 6.3 fusion.56
  1096.0 10.7 fusion.59
  (90 shorter events, 8.7 us)
Async XLA Ops:
  6.5 132.6 %all-gather.17.cloned.1.call-start = ((), (), s32[]{:S(2)}) async-start(), calls=%async_computation | async-start | bytes 28311552 | tf_op jit(solution)/shard_map/all_gather | solution.py:41
  13.3 292.2 %all-gather.21.cloned.1.call-start = ((), (), s32[]{:S(2)}) async-start(), calls=%async_computation.2 | async-start | bytes 37748736 | tf_op jit(solution)/shard_map/all_gather | solution.py:43
  19.5 436.5 %all-gather.23.cloned.1.call-start = ((), (), s32[]{:S(2)}) async-start(), calls=%async_computation.3 | async-start | bytes 37748736 | tf_op jit(solution)/shard_map/all_gather | solution.py:44
  25.4 534.8 %all-gather.19.cloned.1.call-start = ((), (), s32[]{:S(2)}) async-start(), calls=%async_computation.1 | async-start | bytes 9437184 | tf_op jit(solution)/shard_map/all_gather | solution.py:42
  27.1 635.2 %all-gather.29.cloned.1.call-start = ((), (), s32[]{:S(2)}) async-start(), calls=%async_computation.6 | async-start | bytes 37748736 | tf_op jit(solution)/shard_map/all_gather | solution.py:43
  27.7 759.2 %all-gather.25.cloned.1.call-start = ((), (), s32[]{:S(2)}) async-start(), calls=%async_computation.4 | async-start | bytes 28311552 | tf_op jit(solution)/shard_map/all_gather | solution.py:41
  28.3 924.8 %all-gather.31.cloned.1.call-start = ((), (), s32[]{:S(2)}) async-start(), calls=%async_computation.7 | async-start | bytes 37748736 | tf_op jit(solution)/shard_map/all_gather | solution.py:44
  29.1 1028.2 %all-gather.27.cloned.1.call-start = ((), (), s32[]{:S(2)}) async-start(), calls=%async_computation.5 | async-start | bytes 9437184 | tf_op jit(solution)/shard_map/all_gather | solution.py:42
  30.0 225.4 %copy-start.1 = (pred[384,384]{0,1:T(8,128)(4,1)}, pred[384,384]{0,1:T(8,128)(4,1)S(1)}, u32[]{:S(2)}) copy-start(pred[384,384]{0,1:T(8,128)(4,1)S(1)} %iota_compare_fusion) | copy-start | bytes 442372
  35.1 182.0 %copy-start.6 = (f32[6,384]{1,0:T(8,128)}, f32[6,384]{1,0:T(8,128)S(1)}, u32[]{:S(2)}) copy-start(f32[6,384]{1,0:T(8,128)S(1)} %broadcast_multiply_fusion.2) | copy-start | bytes 27652
  41.4 175.7 %copy-start.14 = (f32[6,384]{1,0:T(8,128)}, f32[6,384]{1,0:T(8,128)S(1)}, u32[]{:S(2)}) copy-start(f32[6,384]{1,0:T(8,128)S(1)} %add_rsqrt_fusion.2) | copy-start | bytes 27652
  42.0 175.1 %copy-start.24 = (f32[1,2048]{1,0:T(1,128)}, f32[1,2048]{1,0:T(1,128)S(1)}, u32[]{:S(2)}) copy-start(f32[1,2048]{1,0:T(1,128)S(1)} %get-tuple-element.22) | copy-start | bytes 24580
  42.6 174.5 %copy-start.26 = (f32[1,2048]{1,0:T(1,128)}, f32[1,2048]{1,0:T(1,128)S(1)}, u32[]{:S(2)}) copy-start(f32[1,2048]{1,0:T(1,128)S(1)} %get-tuple-element.24) | copy-start | bytes 24580
  255.4 50.0 %copy-start.7 = (f32[6,384]{1,0:T(8,128)S(1)}, f32[6,384]{1,0:T(8,128)}, u32[]{:S(2)}) copy-start(f32[6,384]{1,0:T(8,128)} %copy-done.6) | copy-start | bytes 27652
  255.4 50.0 %copy-start.15 = (f32[6,384]{1,0:T(8,128)S(1)}, f32[6,384]{1,0:T(8,128)}, u32[]{:S(2)}) copy-start(f32[6,384]{1,0:T(8,128)} %copy-done.14) | copy-start | bytes 27652
  305.5 150.5 %copy-start.9 = (f32[1,8192]{1,0:T(1,128)S(1)}, f32[1,8192]{1,0:T(1,128)}, u32[]{:S(2)}) copy-start(f32[1,8192]{1,0:T(1,128)} %get-tuple-element.16) | copy-start | bytes 98308
  456.0 104.2 %copy-start.22 = (f32[1,2048]{1,0:T(1,128)S(1)}, f32[1,2048]{1,0:T(1,128)}, u32[]{:S(2)}) copy-start(f32[1,2048]{1,0:T(1,128)} %get-tuple-element.18) | copy-start | bytes 24580
  456.0 104.2 %copy-start.23 = (f32[1,2048]{1,0:T(1,128)S(1)}, f32[1,2048]{1,0:T(1,128)}, u32[]{:S(2)}) copy-start(f32[1,2048]{1,0:T(1,128)} %get-tuple-element.20) | copy-start | bytes 24580
  560.2 102.0 %copy-start.20 = (f32[1,2048]{1,0:T(1,128)S(1)}, f32[1,2048]{1,0:T(1,128)}, u32[]{:S(2)}) copy-start(f32[1,2048]{1,0:T(1,128)} %get-tuple-element.21) | copy-start | bytes 24580
  560.2 102.0 %copy-start.21 = (f32[1,2048]{1,0:T(1,128)S(1)}, f32[1,2048]{1,0:T(1,128)}, u32[]{:S(2)}) copy-start(f32[1,2048]{1,0:T(1,128)} %get-tuple-element.23) | copy-start | bytes 24580
  662.2 124.7 %copy-start.5 = (f32[3,32,64]{2,1,0:T(8,128)S(1)}, f32[3,32,64]{2,1,0:T(8,128)}, u32[]{:S(2)}) copy-start(f32[3,32,64]{2,1,0:T(8,128)} %get-tuple-element.13) | copy-start | bytes 73732
  787.0 78.0 %copy-start.2 = (pred[384,384]{0,1:T(8,128)(4,1)S(1)}, pred[384,384]{0,1:T(8,128)(4,1)}, u32[]{:S(2)}) copy-start(pred[384,384]{0,1:T(8,128)(4,1)} %copy-done.1) | copy-start | bytes 442372
  953.1 104.2 %copy-start.18 = (f32[1,2048]{1,0:T(1,128)S(1)}, f32[1,2048]{1,0:T(1,128)}, u32[]{:S(2)}) copy-start(f32[1,2048]{1,0:T(1,128)} %get-tuple-element.17) | copy-start | bytes 24580
  953.1 104.2 %copy-start.19 = (f32[1,2048]{1,0:T(1,128)S(1)}, f32[1,2048]{1,0:T(1,128)}, u32[]{:S(2)}) copy-start(f32[1,2048]{1,0:T(1,128)} %get-tuple-element.19) | copy-start | bytes 24580
  (12 other events, 345.0 us)
Sparse Core Ops, SparseCore 0:
  13.4 125.6 all-gather.16
  140.7 153.5 all-gather.20
  295.9 160.0 all-gather.22
  457.4 49.6 all-gather.18
  508.6 153.5 all-gather.28
  663.6 123.2 all-gather.24
  788.5 160.0 all-gather.30
  950.1 49.6 all-gather.26
where the time goes:
time: 1120 us; the launch traced here: 1110 us
  matrix products  784 us (70%)
  waiting for transfers between devices  257 us (23%)
  other arithmetic  34.6 us (3%)
  local copies, waits for them, and re-layouts  23.8 us (2%)
  between operations  14.3 us (1%)
    dot_general x2, matrix products, decoder_layer(): jnp.einsum('btf,fd->btd', gelu_out, down_weight, preferred_element_type=j...  208 us
    dot_general x2, matrix products, decoder_layer(): jnp.einsum('btd,df->btf', normed, up_weight, preferred_element_type=jnp.f...  179 us
    dot_general x2, matrix products, decoder_layer(): jnp.einsum('btd,dshe->btshe', normed, qkv_weight, preferred_element_type=...  156 us
    all_gather x2, waiting for transfers between devices, local_forward(): full_qkv = lax.all_gather(w_qkv[layer], 'wg', axis=0, tiled=True)  129 us
    dot_general x2, matrix products, decoder_layer(): jnp.einsum('bhqk,bkhe->bqhe', attn_probs, qkv_all[:, :, 2], preferred_ele...  99.9 us
    sub x2, matrix products, decoder_layer(): attn_probs = jax.nn.softmax(scores, axis=-1).astype(jnp.bfloat16)  76.6 us
    dot_general x2, matrix products, decoder_layer(): jnp.einsum('crif,ife->cre', mixed, out_weight, preferred_element_type=jnp...  64.6 us
    all_gather x2, waiting for transfers between devices, local_forward(): full_up = lax.all_gather(w_up[layer], 'wg', axis=0, tiled=True)  63.5 us
  transfers between devices with their start and end apart: 8, of which 4 were waited for; matrix products, arithmetic and copies ran while one was open for 71% of the time, Pallas kernels for 0%

commit v1 on v0

v1 whole, which is shorter than its diff:
```python
import functools

import jax
import jax.numpy as jnp
from jax import lax
from jax.experimental import pallas as pl
from jax.experimental.pallas import tpu as pltpu
from jax.sharding import PartitionSpec as P

EPS = 1e-5
MESH = pl.DeviceIdType.MESH
SLOTS = 7
FLOWS = 9
TO_RIGHT, TO_LEFT, LEFT_AGAIN, PAIR_NEAR, PAIR_FAR, CORE_OWN, CORE_BEFORE, CORE_NEAR, CORE_FAR = range(FLOWS)
FREE_RIGHT, FREE_LEFT, FREE_CORE, FREE_PAIR = range(4)
LOG2_E = 1.4426950408889634


def layer_norm(rows, gain, shift):
    centered = rows - rows.mean(axis=-1, keepdims=True)
    variance = (centered * centered).mean(axis=-1, keepdims=True)
    return centered * lax.rsqrt(variance + EPS) * gain + shift


def dot(lhs, rhs):
    return jnp.dot(lhs, rhs, preferred_element_type=jnp.float32)


def forward_kernel(cfg, hid, wq, wo, wu, wd, bq, bu, bo, gain, shift, last_gain, last_shift, out,
                   acc, act, slots, qkv, mixed, send_sem, recv_sem, load_sem, free_sem, io_sem):
    layers, seqs, seq_len, width, part, head_dim, block, norm_rows = cfg
    parts = width // part
    groups = parts
    chunks = wu.shape[2] // (2 * part)
    per_layer = groups + chunks
    units = layers * per_layer
    half_rows = part // 2

    dp, me = lax.axis_index('dp'), lax.axis_index('wg')
    core = lax.rem(me, 2)
    parity = lax.rem(dp, 2)
    right = (dp, lax.rem(me + 2, parts))
    left = (dp, lax.rem(me + parts - 2, parts))
    partner = (dp, me + 1 - 2 * core)
    pair = (dp + 1 - 2 * parity, me)

    def shard(offset, other=False):
        index = lax.rem(me + parts + offset, parts)
        return index + 1 - 2 * core if other else index

    def piece(unit, index, half=None):
        rows = part if half is None else half_rows
        start = index * part if half is None else index * part + half * half_rows
        return slots.at[lax.rem(unit, SLOTS), pl.ds(pl.multiple_of(start, half_rows), rows), :]

    def remote(flow, unit, ref, target):
        slot = lax.rem(unit, SLOTS)
        return pltpu.make_async_remote_copy(
            src_ref=ref, dst_ref=ref, send_sem=send_sem.at[flow, slot], recv_sem=recv_sem.at[flow, slot],
            device_id=target, device_id_type=MESH)

    def outgoing(flow, unit):
        if flow == TO_RIGHT:
            return remote(flow, unit, piece(unit, me), right)
        if flow == TO_LEFT:
            return remote(flow, unit, piece(unit, me, parity), left)
        if flow == LEFT_AGAIN:
            return remote(flow, unit, piece(unit, shard(2), parity), left)
        if flow == PAIR_NEAR:
            return remote(flow, unit, piece(unit, shard(2), parity), pair)
        if flow == PAIR_FAR:
            return remote(flow, unit, piece(unit, shard(4), parity), pair)
        offset = {CORE_OWN: 0, CORE_BEFORE: -2, CORE_NEAR: 2, CORE_FAR: 4}[flow]
        return remote(flow, unit, piece(unit, shard(offset)), partner)

    def incoming(flow, unit):
        if flow == TO_RIGHT:
            return remote(flow, unit, piece(unit, shard(-2)), right)
        if flow == TO_LEFT:
            return remote(flow, unit, piece(unit, shard(2), parity), left)
        if flow == LEFT_AGAIN:
            return remote(flow, unit, piece(unit, shard(4), parity), left)
        if flow == PAIR_NEAR:
            return remote(flow, unit, piece(unit, shard(2), 1 - parity), pair)
        if flow == PAIR_FAR:
            return remote(flow, unit, piece(unit, shard(4), 1 - parity), pair)
        offset = {CORE_OWN: 0, CORE_BEFORE: -2, CORE_NEAR: 2, CORE_FAR: 4}[flow]
        return remote(flow, unit, piece(unit, shard(offset, other=True)), partner)

    def guarded(stage, unit):
        @pl.when((unit >= 0) & (unit < units))
        def _():
            stage(unit)

    def load_own(unit):
        slot = lax.rem(unit, SLOTS)
        layer, step = unit // per_layer, lax.rem(unit, per_layer)
        rows = pl.ds(pl.multiple_of(me * part, part), part)

        def load(src, first, size):
            pltpu.make_async_copy(src, slots.at[slot, rows, pl.ds(first, size)], load_sem.at[slot]).start()

        @pl.when(step < groups)
        def _():
            load(wq.at[layer, step], 0, 3 * part)
            load(wo.at[layer, pl.ds(pl.multiple_of(step * part, part), part), :], 3 * part, part)

        @pl.when(step >= groups)
        def _():
            first = (step - groups) * 2 * part
            load(wu.at[layer, :, pl.ds(pl.multiple_of(first, 2 * part), 2 * part)], 0, 2 * part)
            for k in range(2):
                load(wd.at[layer, pl.ds(pl.multiple_of(first + k * part, part), part), :], (2 + k) * part, part)

    def send_own(unit):
        ref = piece(unit, me)
        pltpu.make_async_copy(ref, ref, load_sem.at[lax.rem(unit, SLOTS)]).wait()

        @pl.when(unit >= SLOTS)
        def _():
            for which in (FREE_RIGHT, FREE_LEFT, FREE_CORE):
                pl.semaphore_wait(free_sem.at[which], 1)

        for flow in (TO_LEFT, TO_RIGHT, CORE_OWN):
            outgoing(flow, unit).start()

    def pass_near(unit):
        @pl.when(unit >= SLOTS)
        def _():
            pl.semaphore_wait(free_sem.at[FREE_PAIR], 1)

        incoming(TO_LEFT, unit).wait_recv()
        outgoing(LEFT_AGAIN, unit).start()
        outgoing(PAIR_NEAR, unit).start()

    def pass_far(unit):
        incoming(LEFT_AGAIN, unit).wait_recv()
        outgoing(PAIR_FAR, unit).start()
        incoming(TO_RIGHT, unit).wait_recv()
        outgoing(CORE_BEFORE, unit).start()
        incoming(PAIR_NEAR, unit).wait_recv()
        outgoing(CORE_NEAR, unit).start()

    def pass_last(unit):
        incoming(PAIR_FAR, unit).wait_recv()
        outgoing(CORE_FAR, unit).start()

    def arrive(unit):
        for flow in (CORE_OWN, CORE_BEFORE, CORE_NEAR, CORE_FAR):
            incoming(flow, unit).wait_recv()

    def tick(unit):
        guarded(send_own, unit + 5)
        guarded(load_own, unit + 6)
        guarded(pass_last, unit + 1)
        guarded(pass_far, unit + 2)
        guarded(pass_near, unit + 4)
        guarded(arrive, unit)

    def release(unit):
        for flow in range(FLOWS):
            outgoing(flow, unit).wait_send()

        @pl.when(unit + SLOTS < units)
        def _():
            for target, which in ((right, FREE_LEFT), (left, FREE_RIGHT), (partner, FREE_CORE), (pair, FREE_PAIR)):
                pl.semaphore_signal(free_sem.at[which], inc=1, device_id=target, device_id_type=MESH)

    def seq_rows(seq):
        return pl.ds(pl.multiple_of(seq * seq_len, seq_len), seq_len)

    def enter_layer(layer, seq, read):
        def step(i, carry):
            rows = pl.ds(pl.multiple_of(seq * seq_len + i * norm_rows, norm_rows), norm_rows)
            hidden = read(rows).astype(jnp.float32)
            act[rows, :] = layer_norm(hidden, gain[pl.ds(layer, 1), :], shift[pl.ds(layer, 1), :]).astype(jnp.bfloat16)
            acc[rows, :] = hidden + bo[pl.ds(layer, 1), :]
            return carry

        lax.fori_loop(0, seq_len // norm_rows, step, 0)

    causal = (lax.broadcasted_iota(jnp.int32, (block, block), 0)
              >= lax.broadcasted_iota(jnp.int32, (block, block), 1))

    def attention_unit(unit, layer, group):
        w = slots.at[lax.rem(unit, SLOTS)]

        def per_seq(seq, carry):
            rows = seq_rows(seq)
            bias = bq[pl.ds(layer * groups + group, 1), :]
            qkv[...] = (dot(act[rows, :], w[:, :3 * part]) + bias).astype(jnp.bfloat16)
            for head in range(part // head_dim):
                cols = [slice(s * part + head * head_dim, s * part + (head + 1) * head_dim) for s in range(3)]
                for i in range(seq_len // block):
                    mine = slice(i * block, (i + 1) * block)
                    seen = (i + 1) * block
                    scores = lax.dot_general(qkv[mine, cols[0]], qkv[:seen, cols[1]], (((1,), (1,)), ((), ())),
                                             preferred_element_type=jnp.float32)
                    edge = jnp.where(causal, scores[:, i * block:], -1e30)
                    scores = edge if i == 0 else jnp.concatenate([scores[:, :i * block], edge], axis=1)
                    top = scores.max(axis=-1, keepdims=True)
                    weights = jnp.exp2((scores - top) * (head_dim ** -0.5 * LOG2_E))
                    weights = weights * (1.0 / weights.sum(axis=-1, keepdims=True))
                    mixed[mine, head * head_dim:(head + 1) * head_dim] = dot(
                        weights.astype(jnp.bfloat16), qkv[:seen, cols[2]]).astype(jnp.bfloat16)
            for p in range(parts):
                cols = slice(p * part, (p + 1) * part)
                acc[rows, cols] += dot(mixed[...], w[cols, 3 * part:])
            return carry

        lax.fori_loop(0, seqs, per_seq, 0)

    def mlp_unit(unit, layer, chunk):
        w = slots.at[lax.rem(unit, SLOTS)]

        def per_seq(seq, carry):
            rows = seq_rows(seq)
            x = dot(act[rows, :], w[:, :2 * part]) + bu[pl.ds(layer * chunks + chunk, 1), :]
            inner = 0.7978845608028654 * (x + 0.044715 * (x * x * x))
            m = (0.5 * x * (1.0 + jnp.tanh(inner))).astype(jnp.bfloat16)
            for p in range(parts):
                cols = slice(p * part, (p + 1) * part)
                acc[rows, cols] += (dot(m[:, :part], w[cols, 2 * part:3 * part])
                                    + dot(m[:, part:], w[cols, 3 * part:]))
            return carry

        lax.fori_loop(0, seqs, per_seq, 0)

    barrier = pltpu.get_barrier_semaphore()
    for target in (right, left, partner, pair):
        pl.semaphore_signal(barrier, inc=1, device_id=target, device_id_type=MESH)
    read_in = pltpu.make_async_copy(hid, act, io_sem)
    read_in.start()
    load_own(0)
    pl.semaphore_wait(barrier, 4)
    read_in.wait()

    def start_up(i, carry):
        unit = i - 5
        tick(unit)

        @pl.when(i < 5)
        def _():
            enter_layer(0, i, lambda rows: act[rows, :])

        return carry

    lax.fori_loop(0, 5, start_up, 0)
    for seq in range(5, seqs):
        enter_layer(0, seq, lambda rows: act[rows, :])

    def one_layer(layer, carry):
        @pl.when(layer > 0)
        def _():
            def enter(seq, c):
                enter_layer(layer, seq, lambda rows: acc[rows, :].astype(jnp.bfloat16))
                return c

            lax.fori_loop(0, seqs, enter, 0)

        def attention_step(group, c):
            unit = layer * per_layer + group
            tick(unit)
            attention_unit(unit, layer, group)
            release(unit)
            return c

        def mlp_step(chunk, c):
            unit = layer * per_layer + groups + chunk
            tick(unit)
            mlp_unit(unit, layer, chunk)
            release(unit)
            return c

        lax.fori_loop(0, groups, attention_step, 0)
        lax.fori_loop(0, chunks, mlp_step, 0)
        return carry

    lax.fori_loop(0, layers, one_layer, 0)

    def finish(i, carry):
        rows = pl.ds(pl.multiple_of(i * norm_rows, norm_rows), norm_rows)
        hidden = acc[rows, :].astype(jnp.bfloat16).astype(jnp.float32)
        act[rows, :] = layer_norm(hidden, last_gain[...], last_shift[...]).astype(jnp.bfloat16)
        return carry

    lax.fori_loop(0, seqs * seq_len // norm_rows, finish, 0)
    write_out = pltpu.make_async_copy(act, out, io_sem)
    write_out.start()
    write_out.wait()


def solution(mesh):
    row_spec = P(('dp', 'wg'), None, None)
    parts = mesh.shape['wg']

    def local_forward(hidden_in, ln_g, ln_b, w_qkv, b_qkv, w_out, b_out, w_up, b_up, w_down, b_down, lnf_g, lnf_b):
        layers, part, _, heads, head_dim = w_qkv.shape
        seqs, seq_len, width = hidden_in.shape
        ff = w_up.shape[2]
        assert parts == 8 and heads * head_dim == width and part % head_dim == 0
        rows = seqs * seq_len
        block = seq_len // 3
        norm_rows = seq_len // 6
        wq = w_qkv.reshape(layers, part, 3, parts, part).transpose(0, 3, 1, 2, 4).reshape(layers, parts, part, 3 * part)
        bq = b_qkv.reshape(layers, 3, parts, part).transpose(0, 2, 1, 3).reshape(layers * parts, 3 * part)
        bu = b_up.reshape(layers * (ff // (2 * part)), 2 * part)
        vmem = pl.BlockSpec(memory_space=pltpu.VMEM)
        hbm = pl.BlockSpec(memory_space=pl.ANY)
        cfg = (layers, seqs, seq_len, width, part, head_dim, block, norm_rows)
        dma, regular = pltpu.SemaphoreType.DMA, pltpu.SemaphoreType.REGULAR
        out = pl.pallas_call(
            functools.partial(forward_kernel, cfg),
            out_shape=jax.ShapeDtypeStruct((rows, width), jnp.bfloat16),
            in_specs=[hbm] * 5 + [vmem] * 7,
            out_specs=hbm,
            scratch_shapes=[
                pltpu.VMEM((rows, width), jnp.float32),
                pltpu.VMEM((rows, width), jnp.bfloat16),
                pltpu.VMEM((SLOTS, width, 4 * part), jnp.bfloat16),
                pltpu.VMEM((seq_len, 3 * part), jnp.bfloat16),
                pltpu.VMEM((seq_len, part), jnp.bfloat16),
                dma((FLOWS, SLOTS)),
                dma((FLOWS, SLOTS)),
                dma((SLOTS,)),
                regular((4,)),
                dma,
            ],
            compiler_params=pltpu.CompilerParams(
                collective_id=0, has_side_effects=True, vmem_limit_bytes=67_043_328),
            cost_estimate=pl.CostEstimate(
                flops=2 * rows * layers * (4 * width * width + 2 * width * ff),
                bytes_accessed=4 * rows * width, transcendentals=0),
        )(hidden_in.reshape(rows, width), wq, w_out.reshape(layers, width, part), w_up, w_down, bq, bu,
          b_out + b_down, ln_g, ln_b, lnf_g.reshape(1, width), lnf_b.reshape(1, width))
        return out.reshape(seqs, seq_len, width)

    in_specs = (row_spec, P(), P(), P(None, 'wg', None, None, None), P(), P(None, None, None, 'wg'), P(),
                P(None, 'wg', None), P(), P(None, None, 'wg'), P(), P(), P())
    return jax.shard_map(local_forward, mesh=mesh, in_specs=in_specs, out_specs=row_spec, check_vma=False)
```

time: 1120 us -> 1120 us (level)
  Pallas kernels: 0 us -> 1090 us
  matrix products: 784 us -> 0 us
  waiting for transfers between devices: 257 us -> 0 us
  other arithmetic: 34.6 us -> 1.34 us
  between operations: 14.3 us -> 0.01 us
    pallas_call x0 -> x1, Pallas kernels: none -> 1090 us  [local_forward(): pl.pallas_call(functools.partial(forward_kernel, cfg), out_shape=jax.Shap...]
    dot_general x10 -> x0, matrix products: 708 us -> none  [the longest x2 208 us: decoder_layer(): jnp.einsum('btf,fd->btd', gelu_out, down_weight, preferred_element_type=j...]
    all_gather x8 -> x0, waiting for transfers between devices: 254 us -> none  [the longest x2 129 us: local_forward(): full_qkv = lax.all_gather(w_qkv[layer], 'wg', axis=0, tiled=True)]
    sub x2 -> x0, matrix products: 76.6 us -> none  [decoder_layer(): attn_probs = jax.nn.softmax(scores, axis=-1).astype(jnp.bfloat16)]
    reduce_sum x4 -> x0, other arithmetic: 23.9 us -> none  [the longest x3 18.8 us: layer_norm(): variance = (centered * centered).mean(axis=-1, keepdims=True)]
    slice x9 -> x0, local copies, waits for them, and re-layouts: 23.1 us -> none  [the longest x1 6.67 us: local_forward(): full_qkv = lax.all_gather(w_qkv[layer], 'wg', axis=0, tiled=True)]
    reshape x0 -> x3, local copies, waits for them, and re-layouts: none -> 11.8 us  [the longest x1 8.67 us: local_forward(): w_qkv.reshape(layers, part, 3, parts, part).transpose(0, 3, 1, 2, 4)]
  transfers between devices with their start and end apart: 8 -> 0, of which waited for: 4 -> 0; matrix products, arithmetic and copies ran while one was open for 71% -> 0% of each run, Pallas kernels for 0% -> 0%
where the time goes in v1:
time: 1120 us
  Pallas kernels  1090 us (97%)
  local copies, waits for them, and re-layouts  27.3 us (2%)
    pallas_call x1, Pallas kernels, local_forward(): pl.pallas_call(functools.partial(forward_kernel, cfg), out_shape=jax.Shap...  1090 us

profile of v1, /device:TPU:113, one launch (start us, length us, event | category | flops | bytes accessed | tf_op | source)
XLA Modules:
  0.0 1119.9 jit_solution(2951526876273504331)
XLA Ops:
  0.0 1.3 add.3.bo
  1.3 1.6 reshape.34
  2.9 1.5 reshape.36.bu
  4.4 6.2 copy.16
  10.6 8.7 copy.17.wq
  19.3 1091.2 %shard_map.127 = bf16[2304,2048]{1,0:T(8,128)(2,1)} custom-call(bf16[2304,2048]{1,0:T(8,128)(2,1)} %bitcast.18, bf16[2,8,256,768]{3,2,1,0:T(8,128)(2,1)} %copy.17.wq, bf16[2,2048,256]{2,1,0:T(8,128)(2,1)} %bitcast.19, bf16[2,256,8192]{2,1,0:T(8,128)(2,1)} %wu.1, bf16[2,8192,256]{2,1,0:T(8,128)(2,1)} %wd.1, f32[16,768]{1,0:T(8,128)} %bitcast.17, ...), custom_call_target="tpu_custom_call" | custom-call | flops 463856467968 | bytes 18874368 | tf_op jit(solution)/shard_map/pallas_call | solution.py:312
  1110.5 9.4 copy.19

commit v2 on v1

--- a/solution.py
+++ b/solution.py
@@ -14,6 +14,10 @@
 TO_RIGHT, TO_LEFT, LEFT_AGAIN, PAIR_NEAR, PAIR_FAR, CORE_OWN, CORE_BEFORE, CORE_NEAR, CORE_FAR = range(FLOWS)
 FREE_RIGHT, FREE_LEFT, FREE_CORE, FREE_PAIR = range(4)
 LOG2_E = 1.4426950408889634
+GELU_LINEAR = 0.7978845608028654
+GELU_CUBIC = GELU_LINEAR * 0.044715
+AT_ONCE = 2
+MLP_AT_ONCE = 2
 
 
 def layer_norm(rows, gain, shift):
@@ -184,47 +188,86 @@
 
     def attention_unit(unit, layer, group):
         w = slots.at[lax.rem(unit, SLOTS)]
-
-        def per_seq(seq, carry):
+        heads = range(part // head_dim)
+        blocks = range(seq_len // block)
+
+        def project(seq, buf):
+            bias = bq[pl.ds(layer * groups + group, 1), :]
+            qkv[buf] = (dot(act[seq_rows(seq), :], w[:, :3 * part]) + bias).astype(jnp.bfloat16)
+
+        def scores_of(buf, i):
+            mine, seen, scores = slice(i * block, (i + 1) * block), (i + 1) * block, []
+            for head in heads:
+                q, k = (slice(s * part + head * head_dim, s * part + (head + 1) * head_dim) for s in range(2))
+                s = lax.dot_general(qkv[buf, mine, q], qkv[buf, :seen, k], (((1,), (1,)), ((), ())),
+                                    preferred_element_type=jnp.float32)
+                edge = jnp.where(causal, s[:, i * block:], -1e30)
+                scores.append(edge if i == 0 else jnp.concatenate([s[:, :i * block], edge], axis=1))
+            return scores
+
+        def mix(buf, i, scores):
+            mine, seen = slice(i * block, (i + 1) * block), (i + 1) * block
+            tops = [s.max(axis=-1, keepdims=True) for s in scores]
+            weights = [jnp.exp2((s - t) * (head_dim ** -0.5 * LOG2_E)) for s, t in zip(scores, tops)]
+            scales = [1.0 / e.sum(axis=-1, keepdims=True) for e in weights]
+            weights = [(e * c).astype(jnp.bfloat16) for e, c in zip(weights, scales)]
+            outs = [dot(e, qkv[buf, :seen, 2 * part + head * head_dim:2 * part + (head + 1) * head_dim])
+                    for head, e in zip(heads, weights)]
+            mixed[buf, mine, :] = jnp.concatenate([o.astype(jnp.bfloat16) for o in outs], axis=1)
+
+        def attend(buf):
+            ready = scores_of(buf, 0)
+            for i in blocks:
+                later = scores_of(buf, i + 1) if i + 1 < len(blocks) else None
+                mix(buf, i, ready)
+                ready = later
+
+        def project_out(seq, buf):
             rows = seq_rows(seq)
-            bias = bq[pl.ds(layer * groups + group, 1), :]
-            qkv[...] = (dot(act[rows, :], w[:, :3 * part]) + bias).astype(jnp.bfloat16)
-            for head in range(part // head_dim):
-                cols = [slice(s * part + head * head_dim, s * part + (head + 1) * head_dim) for s in range(3)]
-                for i in range(seq_len // block):
-                    mine = slice(i * block, (i + 1) * block)
-                    seen = (i + 1) * block
-                    scores = lax.dot_general(qkv[mine, cols[0]], qkv[:seen, cols[1]], (((1,), (1,)), ((), ())),
-                                             preferred_element_type=jnp.float32)
-                    edge = jnp.where(causal, scores[:, i * block:], -1e30)
-                    scores = edge if i == 0 else jnp.concatenate([scores[:, :i * block], edge], axis=1)
-                    top = scores.max(axis=-1, keepdims=True)
-                    weights = jnp.exp2((scores - top) * (head_dim ** -0.5 * LOG2_E))
-                    weights = weights * (1.0 / weights.sum(axis=-1, keepdims=True))
-                    mixed[mine, head * head_dim:(head + 1) * head_dim] = dot(
-                        weights.astype(jnp.bfloat16), qkv[:seen, cols[2]]).astype(jnp.bfloat16)
             for p in range(parts):
                 cols = slice(p * part, (p + 1) * part)
-                acc[rows, cols] += dot(mixed[...], w[cols, 3 * part:])
+                acc[rows, cols] += dot(mixed[buf], w[cols, 3 * part:])
+
+        def some_seqs(i, carry):
+            first = i * AT_ONCE
+            project(first, 0)
+            for k in range(AT_ONCE):
+                if k + 1 < AT_ONCE:
+                    project(first + k + 1, k + 1)
+                attend(k)
+                project_out(first + k, k)
             return carry
 
-        lax.fori_loop(0, seqs, per_seq, 0)
+        lax.fori_loop(0, seqs // AT_ONCE, some_seqs, 0)
 
     def mlp_unit(unit, layer, chunk):
         w = slots.at[lax.rem(unit, SLOTS)]
 
-        def per_seq(seq, carry):
+        def up(seq):
+            return dot(act[seq_rows(seq), :], w[:, :2 * part]) + bu[pl.ds(layer * chunks + chunk, 1), :]
+
+        def gelu(x):
+            inner = x * (GELU_LINEAR + GELU_CUBIC * (x * x))
+            half = 0.5 * x
+            return (half * jnp.tanh(inner) + half).astype(jnp.bfloat16)
+
+        def down(seq, m):
             rows = seq_rows(seq)
-            x = dot(act[rows, :], w[:, :2 * part]) + bu[pl.ds(layer * chunks + chunk, 1), :]
-            inner = 0.7978845608028654 * (x + 0.044715 * (x * x * x))
-            m = (0.5 * x * (1.0 + jnp.tanh(inner))).astype(jnp.bfloat16)
             for p in range(parts):
                 cols = slice(p * part, (p + 1) * part)
                 acc[rows, cols] += (dot(m[:, :part], w[cols, 2 * part:3 * part])
                                     + dot(m[:, part:], w[cols, 3 * part:]))
+
+        def some_seqs(i, carry):
+            first = i * MLP_AT_ONCE
+            x = up(first)
+            for k in range(MLP_AT_ONCE):
+                later = up(first + k + 1) if k + 1 < MLP_AT_ONCE else None
+                down(first + k, gelu(x))
+                x = later
             return carry
 
-        lax.fori_loop(0, seqs, per_seq, 0)
+        lax.fori_loop(0, seqs // MLP_AT_ONCE, some_seqs, 0)
 
     barrier = pltpu.get_barrier_semaphore()
     for target in (right, left, partner, pair):
@@ -318,8 +361,8 @@
                 pltpu.VMEM((rows, width), jnp.float32),
                 pltpu.VMEM((rows, width), jnp.bfloat16),
                 pltpu.VMEM((SLOTS, width, 4 * part), jnp.bfloat16),
-                pltpu.VMEM((seq_len, 3 * part), jnp.bfloat16),
-                pltpu.VMEM((seq_len, part), jnp.bfloat16),
+                pltpu.VMEM((AT_ONCE, seq_len, 3 * part), jnp.bfloat16),
+                pltpu.VMEM((AT_ONCE, seq_len, part), jnp.bfloat16),
                 dma((FLOWS, SLOTS)),
                 dma((FLOWS, SLOTS)),
                 dma((SLOTS,)),

time: 1120 us -> 760 us (0.68)
  Pallas kernels: 1090 us -> 730 us
    pallas_call x1, Pallas kernels: 1090 us -> 730 us  [local_forward(): pl.pallas_call(functools.partial(forward_kernel, cfg), out_shape=jax.Shap...]
where the time goes in v2:
time: 760 us; the launch traced here: 759 us
  Pallas kernels  730 us (96%)
  local copies, waits for them, and re-layouts  27.3 us (4%)
    pallas_call x1, Pallas kernels, local_forward(): pl.pallas_call(functools.partial(forward_kernel, cfg), out_shape=jax.Shap...  730 us

profile of v2, /device:TPU:113, one launch (start us, length us, event | category | flops | bytes accessed | tf_op | source)
XLA Modules:
  0.0 758.6 jit_solution(14838810150566892168)
XLA Ops:
  0.0 1.3 add.3.bo
  1.3 1.6 reshape.34
  2.9 1.5 reshape.36.bu
  4.4 6.2 copy.16
  10.6 8.7 %copy.17.wq = bf16[2,8,256,768]{3,2,1,0:T(8,128)(2,1)} copy(bf16[2,8,256,768]{2,3,1,0:T(8,128)(2,1)} %bitcast.14) | data formatting | bytes 12582912 | tf_op jit(solution)/shard_map/reshape | solution.py:348
  19.3 729.9 %shard_map.127 = bf16[2304,2048]{1,0:T(8,128)(2,1)} custom-call(bf16[2304,2048]{1,0:T(8,128)(2,1)} %bitcast.18, bf16[2,8,256,768]{3,2,1,0:T(8,128)(2,1)} %copy.17.wq, bf16[2,2048,256]{2,1,0:T(8,128)(2,1)} %bitcast.19, bf16[2,256,8192]{2,1,0:T(8,128)(2,1)} %wu.1, bf16[2,8192,256]{2,1,0:T(8,128)(2,1)} %wd.1, f32[16,768]{1,0:T(8,128)} %bitcast.17, ...), custom_call_target="tpu_custom_call" | custom-call | flops 463856467968 | bytes 18874368 | tf_op jit(solution)/shard_map/pallas_call | solution.py:355
  749.2 9.4 %copy.19 = bf16[6,384,2048]{2,1,0:T(8,128)(2,1)} copy(bf16[6,384,2048]{2,1,0:T(8,128)(2,1)} %bitcast.15) | data formatting | bytes 18874368

commit v3 on v2

--- a/solution.py
+++ b/solution.py
@@ -16,8 +16,7 @@
 LOG2_E = 1.4426950408889634
 GELU_LINEAR = 0.7978845608028654
 GELU_CUBIC = GELU_LINEAR * 0.044715
-AT_ONCE = 2
-MLP_AT_ONCE = 2
+AT_ONCE = 3
 
 
 def layer_norm(rows, gain, shift):
@@ -30,8 +29,9 @@
     return jnp.dot(lhs, rhs, preferred_element_type=jnp.float32)
 
 
-def forward_kernel(cfg, hid, wq, wo, wu, wd, bq, bu, bo, gain, shift, last_gain, last_shift, out,
-                   acc, act, slots, qkv, mixed, send_sem, recv_sem, load_sem, free_sem, io_sem):
+def forward_kernel(cfg, hid, wq, wo, wu, wd, bq, bu, bo, bd, gain, shift, out,
+                   acc, act, slots, qkv, mixed, stage, bias_row,
+                   send_sem, recv_sem, load_sem, free_sem, stage_sem, io_sem):
     layers, seqs, seq_len, width, part, head_dim, block, norm_rows = cfg
     parts = width // part
     groups = parts
@@ -91,23 +91,34 @@
         offset = {CORE_OWN: 0, CORE_BEFORE: -2, CORE_NEAR: 2, CORE_FAR: 4}[flow]
         return remote(flow, unit, piece(unit, shard(offset, other=True)), partner)
 
-    def guarded(stage, unit):
-        @pl.when((unit >= 0) & (unit < units))
-        def _():
-            stage(unit)
+    def place(unit):
+        return unit // per_layer, lax.rem(unit, per_layer)
+
+    def own_rows():
+        return pl.ds(pl.multiple_of(me * part, part), part)
+
+    def start_stage(unit):
+        layer, step = place(unit)
+
+        @pl.when(step < groups)
+        def _():
+            for k in range(3):
+                rows = pl.ds(pl.multiple_of(k * width + step * part, part), part)
+                pltpu.make_async_copy(wq.at[layer, rows, :], stage.at[pl.ds(k * part, part), :], stage_sem).start()
 
     def load_own(unit):
         slot = lax.rem(unit, SLOTS)
-        layer, step = unit // per_layer, lax.rem(unit, per_layer)
-        rows = pl.ds(pl.multiple_of(me * part, part), part)
+        layer, step = place(unit)
 
         def load(src, first, size):
-            pltpu.make_async_copy(src, slots.at[slot, rows, pl.ds(first, size)], load_sem.at[slot]).start()
+            pltpu.make_async_copy(src, slots.at[slot, own_rows(), pl.ds(first, size)], load_sem.at[slot]).start()
 
         @pl.when(step < groups)
         def _():
-            load(wq.at[layer, step], 0, 3 * part)
             load(wo.at[layer, pl.ds(pl.multiple_of(step * part, part), part), :], 3 * part, part)
+            pltpu.make_async_copy(stage, stage, stage_sem).wait()
+            for k in range(3):
+                slots[slot, own_rows(), k * part:(k + 1) * part] = stage[k * part:(k + 1) * part, :].T
 
         @pl.when(step >= groups)
         def _():
@@ -117,8 +128,15 @@
                 load(wd.at[layer, pl.ds(pl.multiple_of(first + k * part, part), part), :], (2 + k) * part, part)
 
     def send_own(unit):
-        ref = piece(unit, me)
-        pltpu.make_async_copy(ref, ref, load_sem.at[lax.rem(unit, SLOTS)]).wait()
+        slot = lax.rem(unit, SLOTS)
+        _, step = place(unit)
+
+        def loaded(cols):
+            ref = slots.at[slot, own_rows(), cols]
+            pltpu.make_async_copy(ref, ref, load_sem.at[slot]).wait()
+
+        pl.when(step < groups)(lambda: loaded(pl.ds(3 * part, part)))
+        pl.when(step >= groups)(lambda: loaded(pl.ds(0, 4 * part)))
 
         @pl.when(unit >= SLOTS)
         def _():
@@ -153,13 +171,34 @@
         for flow in (CORE_OWN, CORE_BEFORE, CORE_NEAR, CORE_FAR):
             incoming(flow, unit).wait_recv()
 
-    def tick(unit):
-        guarded(send_own, unit + 5)
-        guarded(load_own, unit + 6)
-        guarded(pass_last, unit + 1)
-        guarded(pass_far, unit + 2)
-        guarded(pass_near, unit + 4)
-        guarded(arrive, unit)
+    def advance(stage_of, unit, target, most):
+        done, wanted = target(unit - 1), target(unit)
+        for k in range(1, most + 1):
+            later = done + k
+
+            @pl.when((later <= wanted) & (later < units))
+            def _():
+                stage_of(later)
+
+    def tick_first(unit):
+        arrive(unit)
+        advance(send_own, unit, lambda t: jnp.minimum(t + 5, 2 * t + 3 + jnp.where(t < 0, 1, 0)), 2)
+        advance(pass_far, unit, lambda t: t + 1 + jnp.where(t > 2, 1, 0), 2)
+
+        @pl.when((unit > 0) & (unit + 6 < units))
+        def _():
+            load_own(unit + 6)
+
+        @pl.when(unit + 7 < units)
+        def _():
+            start_stage(unit + 7)
+
+    def tick_second(unit):
+        advance(pass_near, unit, lambda t: jnp.minimum(t + 4, 2 * t + 2 + jnp.where(t < 0, 1, 0)), 2)
+
+        @pl.when(unit + 1 < units)
+        def _():
+            pass_last(unit + 1)
 
     def release(unit):
         for flow in range(FLOWS):
@@ -178,7 +217,7 @@
             rows = pl.ds(pl.multiple_of(seq * seq_len + i * norm_rows, norm_rows), norm_rows)
             hidden = read(rows).astype(jnp.float32)
             act[rows, :] = layer_norm(hidden, gain[pl.ds(layer, 1), :], shift[pl.ds(layer, 1), :]).astype(jnp.bfloat16)
-            acc[rows, :] = hidden + bo[pl.ds(layer, 1), :]
+            acc[rows, :] = hidden + (bo[pl.ds(layer, 1), :] + bd[pl.ds(layer, 1), :])
             return carry
 
         lax.fori_loop(0, seq_len // norm_rows, step, 0)
@@ -191,9 +230,13 @@
         heads = range(part // head_dim)
         blocks = range(seq_len // block)
 
+        for k in range(3):
+            for head in heads:
+                row = (layer * 3 + k) * (width // head_dim) + group * len(heads) + head
+                bias_row[:, k * part + head * head_dim:k * part + (head + 1) * head_dim] = bq[pl.ds(row, 1), :]
+
         def project(seq, buf):
-            bias = bq[pl.ds(layer * groups + group, 1), :]
-            qkv[buf] = (dot(act[seq_rows(seq), :], w[:, :3 * part]) + bias).astype(jnp.bfloat16)
+            qkv[buf] = (dot(act[seq_rows(seq), :], w[:, :3 * part]) + bias_row[...]).astype(jnp.bfloat16)
 
         def scores_of(buf, i):
             mine, seen, scores = slice(i * block, (i + 1) * block), (i + 1) * block, []
@@ -230,6 +273,7 @@
 
         def some_seqs(i, carry):
             first = i * AT_ONCE
+            pl.when(i == 1)(lambda: tick_second(unit))
             project(first, 0)
             for k in range(AT_ONCE):
                 if k + 1 < AT_ONCE:
@@ -243,8 +287,10 @@
     def mlp_unit(unit, layer, chunk):
         w = slots.at[lax.rem(unit, SLOTS)]
 
+        bias = bu[pl.ds(layer, 1), pl.ds(pl.multiple_of(chunk * 2 * part, 2 * part), 2 * part)]
+
         def up(seq):
-            return dot(act[seq_rows(seq), :], w[:, :2 * part]) + bu[pl.ds(layer * chunks + chunk, 1), :]
+            return dot(act[seq_rows(seq), :], w[:, :2 * part]) + bias
 
         def gelu(x):
             inner = x * (GELU_LINEAR + GELU_CUBIC * (x * x))
@@ -259,38 +305,55 @@
                                     + dot(m[:, part:], w[cols, 3 * part:]))
 
         def some_seqs(i, carry):
-            first = i * MLP_AT_ONCE
+            first = i * AT_ONCE
+            pl.when(i == 1)(lambda: tick_second(unit))
             x = up(first)
-            for k in range(MLP_AT_ONCE):
-                later = up(first + k + 1) if k + 1 < MLP_AT_ONCE else None
+            for k in range(AT_ONCE):
+                later = up(first + k + 1) if k + 1 < AT_ONCE else None
                 down(first + k, gelu(x))
                 x = later
             return carry
 
-        lax.fori_loop(0, seqs // MLP_AT_ONCE, some_seqs, 0)
+        lax.fori_loop(0, seqs // AT_ONCE, some_seqs, 0)
 
     barrier = pltpu.get_barrier_semaphore()
     for target in (right, left, partner, pair):
         pl.semaphore_signal(barrier, inc=1, device_id=target, device_id_type=MESH)
+    number = [jnp.int32(k) for k in range(SLOTS)]
     read_in = pltpu.make_async_copy(hid, act, io_sem)
+    start_stage(number[0])
     read_in.start()
-    load_own(0)
+    load_own(number[0])
+    start_stage(number[1])
     pl.semaphore_wait(barrier, 4)
+    send_own(number[0])
     read_in.wait()
 
-    def start_up(i, carry):
-        unit = i - 5
-        tick(unit)
-
-        @pl.when(i < 5)
-        def _():
-            enter_layer(0, i, lambda rows: act[rows, :])
-
-        return carry
-
-    lax.fori_loop(0, 5, start_up, 0)
-    for seq in range(5, seqs):
-        enter_layer(0, seq, lambda rows: act[rows, :])
+    def enter_first(first, count):
+        def enter(seq, c):
+            enter_layer(0, seq, lambda rows: act[rows, :])
+            return c
+
+        lax.fori_loop(first, first + count, enter, 0)
+
+    def load_next(unit):
+        load_own(number[unit])
+        if unit + 1 < SLOTS:
+            start_stage(number[unit + 1])
+
+    load_next(1)
+    enter_first(0, 2)
+    pass_near(number[0])
+    send_own(number[1])
+    load_next(2)
+    enter_first(2, 2)
+    pass_far(number[0])
+    pass_near(number[1])
+    send_own(number[2])
+    for unit in range(3, SLOTS):
+        load_next(unit)
+    enter_first(4, seqs - 4)
+    pass_last(number[0])
 
     def one_layer(layer, carry):
         @pl.when(layer > 0)
@@ -303,14 +366,14 @@
 
         def attention_step(group, c):
             unit = layer * per_layer + group
-            tick(unit)
+            tick_first(unit)
             attention_unit(unit, layer, group)
             release(unit)
             return c
 
         def mlp_step(chunk, c):
             unit = layer * per_layer + groups + chunk
-            tick(unit)
+            tick_first(unit)
             mlp_unit(unit, layer, chunk)
             release(unit)
             return c
@@ -321,16 +384,18 @@
 
     lax.fori_loop(0, layers, one_layer, 0)
 
-    def finish(i, carry):
-        rows = pl.ds(pl.multiple_of(i * norm_rows, norm_rows), norm_rows)
-        hidden = acc[rows, :].astype(jnp.bfloat16).astype(jnp.float32)
-        act[rows, :] = layer_norm(hidden, last_gain[...], last_shift[...]).astype(jnp.bfloat16)
+    def finish(seq, carry):
+        rows = seq_rows(seq)
+        act[rows, :] = acc[rows, :].astype(jnp.bfloat16)
+        pltpu.make_async_copy(act.at[rows, :], out.at[rows, :], io_sem).start()
         return carry
 
-    lax.fori_loop(0, seqs * seq_len // norm_rows, finish, 0)
-    write_out = pltpu.make_async_copy(act, out, io_sem)
-    write_out.start()
-    write_out.wait()
+    lax.fori_loop(0, seqs, finish, 0)
+    pltpu.make_async_copy(act, out, io_sem).wait()
+
+
+def last_norm_kernel(hidden, gain, shift, out):
+    out[...] = layer_norm(hidden[...].astype(jnp.float32), gain[...], shift[...]).astype(out.dtype)
 
 
 def solution(mesh):
@@ -345,17 +410,16 @@
         rows = seqs * seq_len
         block = seq_len // 3
         norm_rows = seq_len // 6
-        wq = w_qkv.reshape(layers, part, 3, parts, part).transpose(0, 3, 1, 2, 4).reshape(layers, parts, part, 3 * part)
-        bq = b_qkv.reshape(layers, 3, parts, part).transpose(0, 2, 1, 3).reshape(layers * parts, 3 * part)
-        bu = b_up.reshape(layers * (ff // (2 * part)), 2 * part)
+        wq = w_qkv.transpose(0, 2, 3, 4, 1).reshape(layers, 3 * width, part)
+        bq = b_qkv.reshape(layers * 3 * heads, head_dim)
         vmem = pl.BlockSpec(memory_space=pltpu.VMEM)
         hbm = pl.BlockSpec(memory_space=pl.ANY)
         cfg = (layers, seqs, seq_len, width, part, head_dim, block, norm_rows)
         dma, regular = pltpu.SemaphoreType.DMA, pltpu.SemaphoreType.REGULAR
-        out = pl.pallas_call(
+        hidden = pl.pallas_call(
             functools.partial(forward_kernel, cfg),
             out_shape=jax.ShapeDtypeStruct((rows, width), jnp.bfloat16),
-            in_specs=[hbm] * 5 + [vmem] * 7,
+            in_specs=[hbm] * 5 + [vmem] * 6,
             out_specs=hbm,
             scratch_shapes=[
                 pltpu.VMEM((rows, width), jnp.float32),
@@ -363,10 +427,13 @@
                 pltpu.VMEM((SLOTS, width, 4 * part), jnp.bfloat16),
                 pltpu.VMEM((AT_ONCE, seq_len, 3 * part), jnp.bfloat16),
                 pltpu.VMEM((AT_ONCE, seq_len, part), jnp.bfloat16),
+                pltpu.VMEM((3 * part, part), jnp.bfloat16),
+                pltpu.VMEM((1, 3 * part), jnp.float32),
                 dma((FLOWS, SLOTS)),
                 dma((FLOWS, SLOTS)),
                 dma((SLOTS,)),
                 regular((4,)),
+                dma,
                 dma,
             ],
             compiler_params=pltpu.CompilerParams(
@@ -374,8 +441,18 @@
             cost_estimate=pl.CostEstimate(
                 flops=2 * rows * layers * (4 * width * width + 2 * width * ff),
                 bytes_accessed=4 * rows * width, transcendentals=0),
-        )(hidden_in.reshape(rows, width), wq, w_out.reshape(layers, width, part), w_up, w_down, bq, bu,
-          b_out + b_down, ln_g, ln_b, lnf_g.reshape(1, width), lnf_b.reshape(1, width))
+        )(hidden_in.reshape(rows, width), wq, w_out.reshape(layers, width, part), w_up, w_down, bq, b_up,
+          b_out, b_down, ln_g, ln_b)
+        tile = seq_len // 2
+        one = pl.BlockSpec((1, width), lambda i: (0, 0))
+        tiles = pl.BlockSpec((tile, width), lambda i: (i, 0))
+        out = pl.pallas_call(
+            last_norm_kernel,
+            grid=(rows // tile,),
+            out_shape=jax.ShapeDtypeStruct((rows, width), jnp.bfloat16),
+            in_specs=[tiles, one, one],
+            out_specs=tiles,
+        )(hidden, lnf_g.reshape(1, width), lnf_b.reshape(1, width))
         return out.reshape(seqs, seq_len, width)
 
     in_specs = (row_spec, P(), P(), P(None, 'wg', None, None, None), P(), P(None, None, None, 'wg'), P(),

time: 760 us -> 715 us (0.941)
  local copies, waits for them, and re-layouts: 27.3 us -> 0 us
  Pallas kernels: 730 us -> 714 us
    pallas_call x1, Pallas kernels: 730 us -> 701 us  [local_forward(): pl.pallas_call(functools.partial(forward_kernel, cfg), out_shape=jax.Shap...]
    pallas_call x0 -> x1, Pallas kernels: none -> 13.4 us  [local_forward(): pl.pallas_call(last_norm_kernel, grid=(rows // tile,), out_shape=jax.Shap...]
    reshape x3 -> x0, local copies, waits for them, and re-layouts: 11.8 us -> none  [the longest x1 8.67 us: local_forward(): w_qkv.reshape(layers, part, 3, parts, part).transpose(0, 3, 1, 2, 4)]
    unnamed x1 -> x0, local copies, waits for them, and re-layouts: 9.36 us -> none
where the time goes in v3:
time: 715 us; the launch traced here: 714 us
  Pallas kernels  714 us (100%)
    pallas_call x1, Pallas kernels, local_forward(): pl.pallas_call(functools.partial(forward_kernel, cfg), out_shape=jax.Shap...  701 us

profile of v3, /device:TPU:113, one launch (start us, length us, event | category | flops | bytes accessed | tf_op | source)
XLA Modules:
  0.0 714.5 jit_solution(5182886794735797138)
XLA Ops:
  0.0 701.1 %shard_map.127.hidden = bf16[2304,2048]{1,0:T(8,128)(2,1)} custom-call(bf16[2304,2048]{1,0:T(8,128)(2,1)} %bitcast.11, bf16[2,6144,256]{2,1,0:T(8,128)(2,1)} %bitcast.12, bf16[2,2048,256]{2,1,0:T(8,128)(2,1)} %bitcast.13, bf16[2,256,8192]{2,1,0:T(8,128)(2,1)} %wu.1, bf16[2,8192,256]{2,1,0:T(8,128)(2,1)} %wd.1, f32[192,64]{1,0:T(8,128)} %bitcast.14, ...), custom_call_target="tpu_custom_call" | custom-call | flops 463856467968 | bytes 18874368 | tf_op jit(solution)/shard_map/pallas_call | solution.py:419
  701.1 13.4 %shard_map.128 = bf16[2304,2048]{1,0:T(8,128)(2,1)} custom-call(bf16[2304,2048]{1,0:T(8,128)(2,1)} %shard_map.127.hidden, f32[1,2048]{1,0:T(1,128)} %bitcast.9, f32[1,2048]{1,0:T(1,128)} %bitcast.10), custom_call_target="tpu_custom_call" | custom-call | tf_op jit(solution)/shard_map/pallas_call | solution.py:449
